TPU v7x, 32 devices: a whole 2x2x4 slice. The times are simulated.
32 devices in a mesh: ctx: 4 (over y, x), fsdp: 8 (over z, core).
Axes of the slice: x: 2, y: 2, z: 4, core: 2. Of those that a mesh axis runs over, the one named last changes fastest.
Arguments:
- hidden_in: bfloat16 [8, 512, 2048], P('fsdp', 'ctx'), may hold values from -6 to 6
- block_order: int32 [8, 8], P('fsdp'), may hold values from 0 to 7, each once within a row
- w_query: bfloat16 [2048, 2048], P('fsdp'), may hold values from -0.125 to 0.125
- w_key: bfloat16 [2048, 2048], P('fsdp'), may hold values from -0.125 to 0.125
- w_value: bfloat16 [2048, 2048], P('fsdp'), may hold values from -0.125 to 0.125
- w_output: bfloat16 [2048, 2048], P('fsdp'), may hold values from -0.125 to 0.125
- w_gate: bfloat16 [2048, 8192], P(None, 'fsdp'), may hold values from -0.125 to 0.125
- w_up: bfloat16 [2048, 8192], P(None, 'fsdp'), may hold values from -0.125 to 0.125
- w_down: bfloat16 [8192, 2048], P('fsdp'), may hold values from -0.0625 to 0.0625
- norm_gains: bfloat16 [4, 2048], P(None, 'fsdp'), may hold values from 0.3 to 5.5
- out_grad: bfloat16 [8, 512, 2048], P('fsdp', 'ctx'), may hold values from -6 to 6
Outputs:
- block_out: bfloat16 [8, 512, 2048], P('fsdp', 'ctx')
- input_grad: float32 [8, 512, 2048], P('fsdp', 'ctx')
- grad_query: float32 [2048, 2048], P('fsdp')
- grad_key: float32 [2048, 2048], P('fsdp')
- grad_value: float32 [2048, 2048], P('fsdp')
- grad_output: float32 [2048, 2048], P('fsdp')
- grad_gate: float32 [2048, 8192], P(None, 'fsdp')
- grad_up: float32 [2048, 8192], P(None, 'fsdp')
- grad_down: float32 [8192, 2048], P('fsdp')
- grad_gains: float32 [4, 2048], P(None, 'fsdp')
Inputs may be any that keep to these rules, and one draw needn't show every extreme that they name: `block_order`: each row names every block 0 to 7 once; entry j is the block of that sequence held in rows j * 64 to (j + 1) * 64 - 1.
All inputs are finite; a program needn't handle non-finite values.
Results may differ from a plain program's by a relative error of at most 0.023.
The roundings to bfloat16 on the way count: a program that leaves them out, or rounds other values in their place, can miss the bound.
Values may be sent and summed in bfloat16 or wider, within the bound.
A program may use at most 320 MiB of HBM per device.

v0:
```python
import jax
import jax.numpy as jnp
from jax import lax
from jax.sharding import PartitionSpec as P

HEADS = 16
HEAD_DIM = 128
norm_eps = 1e-06
rope_base = 500000.0
neg_fill = -1e30


def norm_stat(values):
    return lax.rsqrt(jnp.mean(values * values, axis=-1, keepdims=True) + norm_eps)


def norm_back(values, scale, gain, grad_out):
    weighted = grad_out * gain
    grad_values = scale * weighted - values * (scale * scale * scale) * jnp.mean(
        weighted * values, axis=-1, keepdims=True
    )
    grad_gain = jnp.sum(grad_out * (values * scale), axis=0)
    return (grad_values, grad_gain)


def rotate_half(values):
    half_width = values.shape[-1] // 2
    return jnp.concatenate([-values[..., half_width:], values[..., :half_width]], axis=-1)


def rope_tables(positions, width):
    half_width = width // 2
    inverse = rope_base ** (-(jnp.arange(half_width, dtype=jnp.float32) * 2.0) / width)
    angle = positions.astype(jnp.float32)[:, None] * inverse[None, :]
    cosine = jnp.concatenate([jnp.cos(angle), jnp.cos(angle)], axis=-1)
    sine = jnp.concatenate([jnp.sin(angle), jnp.sin(angle)], axis=-1)
    return (cosine[:, None, :], sine[:, None, :])


def apply_rope(values, cosine, sine):
    shaped = values.reshape(values.shape[0], HEADS, HEAD_DIM)
    return shaped * cosine + rotate_half(shaped) * sine


def rope_back(grads, cosine, sine):
    shaped = grads.reshape(grads.shape[0], HEADS, HEAD_DIM)
    return (shaped * cosine - rotate_half(shaped * sine)).reshape(grads.shape)


def shards(
    hidden_in,
    block_order,
    w_query,
    w_key,
    w_value,
    w_output,
    w_gate,
    w_up,
    w_down,
    norm_gains,
    out_grad,
):
    num_rows = hidden_in.shape[1]
    width = hidden_in.shape[2]
    block_rows = num_rows // 2
    seq_rows = num_rows * lax.axis_size("ctx")
    score_scale = HEAD_DIM ** (-0.5)
    tokens_b = hidden_in[0]
    tokens_f = tokens_b.astype(jnp.float32)
    full_query, full_key, full_value, full_output, gains_b = (
        lax.all_gather(w_query, "fsdp", axis=0, tiled=True),
        lax.all_gather(w_key, "fsdp", axis=0, tiled=True),
        lax.all_gather(w_value, "fsdp", axis=0, tiled=True),
        lax.all_gather(w_output, "fsdp", axis=0, tiled=True),
        lax.all_gather(norm_gains, "fsdp", axis=1, tiled=True),
    )
    gains = gains_b.astype(jnp.float32)
    offsets = jnp.arange(block_rows, dtype=jnp.int32)
    all_pos = (block_order[0][:, None] * block_rows + offsets[None, :]).reshape(seq_rows)
    own_pos = lax.dynamic_slice_in_dim(all_pos, lax.axis_index("ctx") * num_rows, num_rows)
    cosine, sine = rope_tables(own_pos, HEAD_DIM)
    query_raw = jnp.dot(tokens_b, full_query, preferred_element_type=jnp.float32)
    key_raw = jnp.dot(tokens_b, full_key, preferred_element_type=jnp.float32)
    query_scale = norm_stat(query_raw)
    key_scale = norm_stat(key_raw)
    query_heads = apply_rope(query_raw * query_scale * gains[0], cosine, sine).astype(jnp.bfloat16)
    key_b = (
        apply_rope(key_raw * key_scale * gains[1], cosine, sine)
        .astype(jnp.bfloat16)
        .reshape(num_rows, width)
    )
    value_b = jnp.dot(tokens_b, full_value, preferred_element_type=jnp.float32).astype(jnp.bfloat16)
    key_all, value_all = (
        lax.all_gather(key_b, "ctx", axis=0, tiled=True),
        lax.all_gather(value_b, "ctx", axis=0, tiled=True),
    )
    query_major = query_heads.transpose(1, 0, 2)
    key_major = key_all.reshape(seq_rows, HEADS, HEAD_DIM).transpose(1, 0, 2)
    value_major = value_all.reshape(seq_rows, HEADS, HEAD_DIM).transpose(1, 0, 2)
    allowed = all_pos[None, :] <= own_pos[:, None]

    def head_scores(query_one, key_one):
        raw_scores = jnp.dot(query_one, key_one.T, preferred_element_type=jnp.float32) * score_scale
        return jnp.where(allowed, raw_scores, neg_fill)

    def head_forward(items):
        query_one, key_one, value_one = items
        scores = head_scores(query_one, key_one)
        peak = jnp.max(scores, axis=-1, keepdims=True)
        expd = jnp.exp(scores - peak)
        denom = jnp.sum(expd, axis=-1, keepdims=True)
        probs = expd / denom
        mixed_one = jnp.dot(
            probs.astype(jnp.bfloat16), value_one, preferred_element_type=jnp.float32
        )
        return (mixed_one, peak + jnp.log(denom))

    mixed_major, log_total = lax.map(head_forward, (query_major, key_major, value_major))
    mixed_b = mixed_major.transpose(1, 0, 2).reshape(num_rows, width).astype(jnp.bfloat16)
    projected = jnp.dot(mixed_b, full_output, preferred_element_type=jnp.float32)
    proj_scale = norm_stat(projected)
    residual = tokens_f + projected * proj_scale * gains[2]
    residual_b = residual.astype(jnp.bfloat16)
    gate_w, up_w, down_w = (w_gate, w_up, w_down)
    mlp_rows_in = lax.all_gather(residual_b, "fsdp", axis=0, tiled=True)
    gate = jnp.dot(mlp_rows_in, gate_w, preferred_element_type=jnp.float32)
    upward = jnp.dot(mlp_rows_in, up_w, preferred_element_type=jnp.float32)
    sigma = jax.nn.sigmoid(gate)
    hidden_b = (gate * sigma * upward).astype(jnp.bfloat16)
    partial_out = jnp.dot(hidden_b, down_w, preferred_element_type=jnp.float32)
    mlp_out = lax.psum_scatter(partial_out, "fsdp", scatter_dimension=0, tiled=True)
    mlp_scale = norm_stat(mlp_out)
    block_out = residual + mlp_out * mlp_scale * gains[3]
    grad_y = out_grad[0].astype(jnp.float32)
    grad_mlp, gain_ff = norm_back(mlp_out, mlp_scale, gains[3], grad_y)
    grad_mlp_b = grad_mlp.astype(jnp.bfloat16)
    grad_rows = lax.all_gather(grad_mlp_b, "fsdp", axis=0, tiled=True)
    grad_hidden = jnp.dot(grad_rows, down_w.T, preferred_element_type=jnp.float32)
    grad_gate_b = (grad_hidden * upward * sigma * (1.0 + gate * (1.0 - sigma))).astype(jnp.bfloat16)
    grad_up_b = (grad_hidden * (gate * sigma)).astype(jnp.bfloat16)
    back_part = jnp.dot(grad_gate_b, gate_w.T, preferred_element_type=jnp.float32) + jnp.dot(
        grad_up_b, up_w.T, preferred_element_type=jnp.float32
    )
    grad_mlp_in = lax.psum_scatter(back_part, "fsdp", scatter_dimension=0, tiled=True)
    gate_grad_own = jnp.dot(mlp_rows_in.T, grad_gate_b, preferred_element_type=jnp.float32)
    up_grad_own = jnp.dot(mlp_rows_in.T, grad_up_b, preferred_element_type=jnp.float32)
    down_grad_own = jnp.dot(hidden_b.T, grad_rows, preferred_element_type=jnp.float32)
    grad_res = grad_y + grad_mlp_in
    grad_proj, gain_attn = norm_back(projected, proj_scale, gains[2], grad_res)
    grad_proj_b = grad_proj.astype(jnp.bfloat16)
    grad_mixed_b = jnp.dot(grad_proj_b, full_output.T, preferred_element_type=jnp.float32).astype(
        jnp.bfloat16
    )
    grad_mixed_major = grad_mixed_b.reshape(num_rows, HEADS, HEAD_DIM).transpose(1, 0, 2)

    def head_backward(items):
        query_one, key_one, value_one, grad_one, total_one = items
        probs_again = jnp.exp(head_scores(query_one, key_one) - total_one)
        grad_probs = jnp.dot(grad_one, value_one.T, preferred_element_type=jnp.float32)
        grad_value_one = jnp.dot(
            probs_again.astype(jnp.bfloat16).T, grad_one, preferred_element_type=jnp.float32
        )
        grad_scores_b = (
            probs_again * (grad_probs - jnp.sum(probs_again * grad_probs, axis=-1, keepdims=True))
        ).astype(jnp.bfloat16)
        grad_query_one = (
            jnp.dot(grad_scores_b, key_one, preferred_element_type=jnp.float32) * score_scale
        )
        grad_key_one = (
            jnp.dot(grad_scores_b.T, query_one, preferred_element_type=jnp.float32) * score_scale
        )
        return (grad_query_one, grad_key_one, grad_value_one)

    grad_query_major, grad_key_major, grad_value_major = lax.map(
        head_backward, (query_major, key_major, value_major, grad_mixed_major, log_total)
    )
    grad_queries = grad_query_major.transpose(1, 0, 2).reshape(num_rows, width)
    grad_key_all = grad_key_major.transpose(1, 0, 2).reshape(seq_rows, width)
    grad_value_all = grad_value_major.transpose(1, 0, 2).reshape(seq_rows, width)
    grad_keys, grad_values = (
        lax.psum_scatter(grad_key_all, "ctx", scatter_dimension=0, tiled=True),
        lax.psum_scatter(grad_value_all, "ctx", scatter_dimension=0, tiled=True),
    )
    grad_value_b = grad_values.astype(jnp.bfloat16)
    grad_key_raw, gain_key = norm_back(
        key_raw, key_scale, gains[1], rope_back(grad_keys, cosine, sine)
    )
    grad_query_raw, gain_query = norm_back(
        query_raw, query_scale, gains[0], rope_back(grad_queries, cosine, sine)
    )
    grad_key_b = grad_key_raw.astype(jnp.bfloat16)
    grad_query_b = grad_query_raw.astype(jnp.bfloat16)
    input_grad = grad_res + jnp.dot(grad_query_b, full_query.T, preferred_element_type=jnp.float32)
    input_grad = input_grad + jnp.dot(grad_key_b, full_key.T, preferred_element_type=jnp.float32)
    input_grad = input_grad + jnp.dot(
        grad_value_b, full_value.T, preferred_element_type=jnp.float32
    )
    stacked_in = jnp.concatenate([grad_query_b, grad_key_b, grad_value_b], axis=1)
    attn_stack = lax.psum_scatter(
        jnp.concatenate(
            [
                jnp.dot(tokens_b.T, stacked_in, preferred_element_type=jnp.float32),
                jnp.dot(mixed_b.T, grad_proj_b, preferred_element_type=jnp.float32),
            ],
            axis=1,
        ).astype(jnp.bfloat16),
        "fsdp",
        scatter_dimension=0,
        tiled=True,
    )
    gain_stack = jnp.stack([gain_query, gain_key, gain_attn, gain_ff], axis=0)
    gain_total = lax.psum(gain_stack, ("ctx", "fsdp"))
    gain_width = gain_total.shape[1] // lax.axis_size("fsdp")
    gain_own = lax.dynamic_slice_in_dim(
        gain_total, lax.axis_index("fsdp") * gain_width, gain_width, 1
    )
    attn_summed, gate_summed, up_summed, down_summed = (
        lax.psum(attn_stack, "ctx").astype(jnp.float32),
        lax.psum(gate_grad_own.astype(jnp.bfloat16), "ctx").astype(jnp.float32),
        lax.psum(up_grad_own.astype(jnp.bfloat16), "ctx").astype(jnp.float32),
        lax.psum(down_grad_own.astype(jnp.bfloat16), "ctx").astype(jnp.float32),
    )
    return (
        block_out.astype(jnp.bfloat16)[None],
        input_grad[None],
        attn_summed[:, :width],
        attn_summed[:, width : 2 * width],
        attn_summed[:, 2 * width : 3 * width],
        attn_summed[:, 3 * width :],
        gate_summed,
        up_summed,
        down_summed,
        gain_own,
    )


def solution(mesh):
    return jax.shard_map(
        shards,
        mesh=mesh,
        in_specs=(
            P("fsdp", "ctx", None),
            P("fsdp", None),
            P("fsdp", None),
            P("fsdp", None),
            P("fsdp", None),
            P("fsdp", None),
            P(None, "fsdp"),
            P(None, "fsdp"),
            P("fsdp", None),
            P(None, "fsdp"),
            P("fsdp", "ctx", None),
        ),
        out_specs=(
            P("fsdp", "ctx", None),
            P("fsdp", "ctx", None),
            P("fsdp", None),
            P("fsdp", None),
            P("fsdp", None),
            P("fsdp", None),
            P(None, "fsdp"),
            P(None, "fsdp"),
            P("fsdp", None),
            P(None, "fsdp"),
        ),
        check_vma=False,
    )
```

profile of v0, /device:TPU:0, one launch (start us, length us, event | category | flops | bytes accessed | tf_op | source)
XLA Modules:
  0.0 1702.8 jit_solution(14575378265479232911)
XLA Ops:
  10.3 14.6 all_gather.28
  25.4 69.0 %all-gather.15.cloned.1.call-done = bf16[2048,2048]{1,0:T(8,128)(2,1)} async-done(((bf16[256,2048]{1,0:T(8,128)(2,1)}), bf16[2048,2048]{1,0:T(8,128)(2,1)}) %all-gather.15.cloned.1.call-update) | async-done | bytes 8388624 | tf_op jit(solution)/shard_map/all_gather | solution.py:73
  99.9 76.6 %all-gather.11.cloned.1.call-done = bf16[2048,2048]{1,0:T(8,128)(2,1)} async-done(((bf16[256,2048]{1,0:T(8,128)(2,1)}), bf16[2048,2048]{1,0:T(8,128)(2,1)}) %all-gather.11.cloned.1.call-update) | async-done | bytes 8388624 | tf_op jit(solution)/shard_map/all_gather | solution.py:72
  184.2 74.4 %all-gather.9.cloned.1.call-done = bf16[2048,2048]{1,0:T(8,128)(2,1)} async-done(((bf16[256,2048]{1,0:T(8,128)(2,1)}), bf16[2048,2048]{1,0:T(8,128)(2,1)}) %all-gather.9.cloned.1.call-update) | async-done | bytes 8388624 | tf_op jit(solution)/shard_map/all_gather | solution.py:71
  269.3 25.3 %all-gather.17.cloned.1.call-done = bf16[512,2048]{1,0:T(8,128)(2,1)} async-done(((bf16[128,2048]{1,0:T(8,128)(2,1)}), bf16[512,2048]{1,0:T(8,128)(2,1)}) %all-gather.17.cloned.1.call-update) | async-done | bytes 2097168 | tf_op jit(solution)/shard_map/all_gather | solution.py:95
  298.1 34.0 %all-gather.13.cloned.1.call-done = bf16[512,2048]{1,0:T(8,128)(2,1)} async-done(((bf16[128,2048]{1,0:T(8,128)(2,1)}), bf16[512,2048]{1,0:T(8,128)(2,1)}) %all-gather.13.cloned.1.call-update) | async-done | bytes 2097168 | tf_op jit(solution)/shard_map/all_gather | solution.py:94
  335.6 42.3 %while.28 = (s32[]{:T(128)}, bf16[16,128,128]{1,2,0:T(8,128)(2,1)S(1)}, f32[16,128,1]{1,2,0:T(1,128)S(1)}, bf16[16,128,128]{2,1,0:T(8,128)(2,1)}, bf16[16,512,12...) while((s32[]{:T(128)}, ...), condition=%wide.region_5.6_spmd.clone, body=%wide.region_2.5_spmd.clone.sunk | while | flops 34144128 | bytes 1155689 | solution.py:118
  377.9 37.7 %all-gather.19.cloned.1.call-done = bf16[2048,2048]{1,0:T(8,128)(2,1)} async-done(((bf16[256,2048]{1,0:T(8,128)(2,1)}), bf16[2048,2048]{1,0:T(8,128)(2,1)}) %all-gather.19.cloned.1.call-update) | async-done | bytes 8388624 | tf_op jit(solution)/shard_map/all_gather | solution.py:74
  422.7 45.3 %all-gather.21.cloned.1.call-done = bf16[1024,2048]{1,0:T(8,128)(2,1)} async-done(((bf16[128,2048]{1,0:T(8,128)(2,1)}), bf16[1024,2048]{1,0:T(8,128)(2,1)}) %all-gather.21.cloned.1.call-update) | async-done | bytes 4194320 | tf_op jit(solution)/shard_map/all_gather | solution.py:125
  468.0 7.7 fusion.85
  475.7 6.5 multiply_convert_fusion.3
  483.5 6.7 fusion.86
  490.2 88.4 %reduce-scatter.6.cloned.1.call-done = f32[128,2048]{1,0:T(8,128)} async-done(((f32[1024,2048]{1,0:T(8,128)}), f32[128,2048]{1,0:T(8,128)}) %reduce-scatter.6.cloned.1.call-update) | async-done | bytes 1048592 | tf_op jit(solution)/shard_map/reduce_scatter | solution.py:131
  584.4 45.0 %all-gather.23.cloned.1.call-done = bf16[1024,2048]{1,0:T(8,128)(2,1)} async-done(((bf16[128,2048]{1,0:T(8,128)(2,1)}), bf16[1024,2048]{1,0:T(8,128)(2,1)}) %all-gather.23.cloned.1.call-update) | async-done | bytes 4194320 | tf_op jit(solution)/shard_map/all_gather | solution.py:137
  629.5 13.0 multiply_convert_fusion.1
  642.5 7.0 fusion.87
  649.5 6.8 convolution_add_fusion
  656.6 88.3 %reduce-scatter.8.cloned.1.call-done = f32[128,2048]{1,0:T(8,128)} async-done(((f32[1024,2048]{1,0:T(8,128)}), f32[128,2048]{1,0:T(8,128)}) %reduce-scatter.8.cloned.1.call-update) | async-done | bytes 1048592 | tf_op jit(solution)/shard_map/reduce_scatter | solution.py:144
  750.0 6.5 fusion.56
  757.4 120.4 %while.29 = (s32[]{:T(128)}, f32[16,128,128]{2,1,0:T(8,128)}, f32[16,512,128]{2,1,0:T(8,128)}, f32[16,512,128]{2,1,0:T(8,128)}, bf16[16,128,128]{2,1,0:T(8,128)(...) while((s32[]{:T(128)}, f32[16,128,128]{2,1,0:T(8,128)}, ...), condition=%wide.region_14.15_spmd.clone, body=%wide.region_12.14_spmd.clone.sunk | while | flops 84623232 | bytes 3090561 | solution.py:174
  897.4 36.3 %reduce-scatter.10.cloned.1.call-done = f32[128,2048]{1,0:T(8,128)} async-done(((f32[512,2048]{1,0:T(8,128)}), f32[128,2048]{1,0:T(8,128)}) %reduce-scatter.10.cloned.1.call-update) | async-done | bytes 1048592 | tf_op jit(solution)/shard_map/reduce_scatter | solution.py:181
  936.8 52.9 %reduce-scatter.12.cloned.1.call-done = f32[128,2048]{1,0:T(8,128)} async-done(((f32[512,2048]{1,0:T(8,128)}), f32[128,2048]{1,0:T(8,128)}) %reduce-scatter.12.cloned.1.call-update) | async-done | bytes 1048592 | tf_op jit(solution)/shard_map/reduce_scatter | solution.py:182
  991.1 11.8 convert_bitcast_fusion
  1002.9 23.9 %pad_maximum_fusion = bf16[2048,8192]{0,1:T(8,128)(2,1)} fusion(bf16[2048,2048]{0,1:T(8,128)(2,1)} %convolution_convert_fusion, bf16[2048,6144]{0,1:T(8,128)(2,1)} %convert_bitcast_fusion), kind=kLoop, calls=%fused_computation.57 | loop fusion | flops 67108864 | bytes 67108864 | tf_op jit(solution)/shard_map/concatenate | solution.py:200
  1027.1 9.6 convolution_convert_fusion.1
  1049.1 303.3 %reduce-scatter.14.cloned.1.call-done = bf16[256,8192]{0,1:T(8,128)(2,1)} async-done(((bf16[2048,8192]{0,1:T(8,128)(2,1)}), bf16[256,8192]{0,1:T(8,128)(2,1)}) %reduce-scatter.14.cloned.1.call-update) | async-done | bytes 4194320 | tf_op jit(solution)/shard_map/reduce_scatter | solution.py:199
  1353.7 7.2 convolution_add_fusion.3
  1361.0 39.4 %psum.39 = f32[4,2048]{1,0:T(4,128)S(1)} all-reduce(f32[4,2048]{1,0:T(4,128)S(1)} %pad_maximum_fusion.3), channel_id=1, replica_groups=mesh['ctx'=4,'fsdp'=8] {'ctx','fsdp'}, use_global_device_ids=true, to_apply=%region_28.29 | all-reduce | flops 8192 | bytes 65536 | tf_op jit(solution)/shard_map/psum | solution.py:212
  1401.0 6.9 convolution_add_fusion.2
  1407.9 7.3 fusion.48
  1415.2 249.5 %all-reduce.3.cloned.1.call-done = (bf16[256,8192]{0,1:T(8,128)(2,1)}, bf16[2048,1024]{1,0:T(8,128)(2,1)}, bf16[2048,1024]{1,0:T(8,128)(2,1)}, bf16[1024,2048]{1,0:T(8,128)(2,1)}) async-done(((bf16[256,8192]{0,1:T(8,128)(2,1)}, bf16[2048,1024]{1,0:T(8,128)(2,1)}, bf16[2048,1024]{1,0:T(8,128)(2,1)}, bf16[1024,2048]{1,0:T(8,128)(2,1)}), (bf16[256,8192]{0,1:T(8,128)(2,1)}, bf16[2048,1024]{1,0:T(8,128)(2,1)}, ...) | async-done | bytes 16777232 | tf_op jit(solution)/shard_map/psum | solution.py:218
  1680.2 6.8 convert_element_type.122
  (326 shorter events, 279.6 us)
Async XLA Ops:
  7.2 87.2 %copy-start = (bf16[1,128,2048]{2,1,0:T(8,128)(2,1)S(1)}, bf16[1,128,2048]{2,1,0:T(8,128)(2,1)}, u32[]{:S(2)}) copy-start(bf16[1,128,2048]{2,1,0:T(8,128)(2,1)} %param.15) | copy-start | bytes 1572868
  7.2 87.2 %all-gather.15.cloned.1.call-start = ((), (), s32[]{:S(2)}) async-start(), calls=%async_computation.8 | async-start | bytes 9437184 | tf_op jit(solution)/shard_map/all_gather | solution.py:73
  7.9 168.6 %all-gather.11.cloned.1.call-start = ((), (), s32[]{:S(2)}) async-start(), calls=%async_computation.6 | async-start | bytes 9437184 | tf_op jit(solution)/shard_map/all_gather | solution.py:72
  8.7 250.0 %all-gather.9.cloned.1.call-start = ((), (), s32[]{:S(2)}) async-start(), calls=%async_computation.5 | async-start | bytes 9437184 | tf_op jit(solution)/shard_map/all_gather | solution.py:71
  9.4 285.3 %all-gather.17.cloned.1.call-start = ((), (), s32[]{:S(2)}) async-start(), calls=%async_computation.9 | async-start | bytes 2621440 | tf_op jit(solution)/shard_map/all_gather | solution.py:95
  99.8 232.3 %all-gather.13.cloned.1.call-start = ((), (), s32[]{:S(2)}) async-start(), calls=%async_computation.7 | async-start | bytes 2621440 | tf_op jit(solution)/shard_map/all_gather | solution.py:94
  258.7 5.0 copy-start.16
  268.7 147.0 %all-gather.19.cloned.1.call-start = ((), (), s32[]{:S(2)}) async-start(), calls=%async_computation.10 | async-start | bytes 9437184 | tf_op jit(solution)/shard_map/all_gather | solution.py:74
  269.3 198.7 %all-gather.21.cloned.1.call-start = ((), (), s32[]{:S(2)}) async-start(), calls=%async_computation.11 | async-start | bytes 4718592 | tf_op jit(solution)/shard_map/all_gather | solution.py:125
  377.9 42.5 %copy-start.10 = (bf16[16,128,128]{1,2,0:T(8,128)(2,1)}, bf16[16,128,128]{1,2,0:T(8,128)(2,1)S(1)}, u32[]{:S(2)}) copy-start(bf16[16,128,128]{1,2,0:T(8,128)(2,1)S(1)} %get-tuple-element.102) | copy-start | bytes 1572868
  422.4 156.2 %reduce-scatter.6.cloned.1.call-start = ((), (), s32[]{:S(2)}) async-start(), calls=%async_computation.12 | async-start | bytes 9437184 | tf_op jit(solution)/shard_map/reduce_scatter | solution.py:131
  468.0 7.7 copy-start.19
  468.0 7.7 copy-start.21
  475.7 6.5 copy-start.26
  475.7 7.8 copy-start.17
  490.2 89.9 %copy-start.2 = (bf16[1,128,2048]{2,1,0:T(8,128)(2,1)S(1)}, bf16[1,128,2048]{2,1,0:T(8,128)(2,1)}, u32[]{:S(2)}) copy-start(bf16[1,128,2048]{2,1,0:T(8,128)(2,1)} %param.25) | copy-start | bytes 1572868
  490.2 139.3 %all-gather.23.cloned.1.call-start = ((), (), s32[]{:S(2)}) async-start(), calls=%async_computation.13 | async-start | bytes 4718592 | tf_op jit(solution)/shard_map/all_gather | solution.py:137
  584.0 160.9 %reduce-scatter.8.cloned.1.call-start = ((), (), s32[]{:S(2)}) async-start(), calls=%async_computation.14 | async-start | bytes 9437184 | tf_op jit(solution)/shard_map/reduce_scatter | solution.py:144
  629.5 13.0 copy-start.18
  642.5 7.0 copy-start.24
  642.5 7.0 copy-start.20
  656.3 277.4 %reduce-scatter.10.cloned.1.call-start = ((), (), s32[]{:S(2)}) async-start(), calls=%async_computation.15 | async-start | bytes 5242880 | tf_op jit(solution)/shard_map/reduce_scatter | solution.py:181
  750.0 6.5 copy-start.8
  882.5 107.2 %reduce-scatter.12.cloned.1.call-start = ((), (), s32[]{:S(2)}) async-start(), calls=%async_computation.16 | async-start | bytes 5242880 | tf_op jit(solution)/shard_map/reduce_scatter | solution.py:182
  887.4 465.1 %reduce-scatter.14.cloned.1.call-start = ((), (), s32[]{:S(2)}) async-start(), calls=%async_computation.17 | async-start | bytes 37748736 | tf_op jit(solution)/shard_map/reduce_scatter | solution.py:199
  935.6 55.5 %copy-start.7 = (bf16[128,2048]{1,0:T(8,128)(2,1)S(1)}, bf16[128,2048]{1,0:T(8,128)(2,1)}, u32[]{:S(2)}) copy-start(bf16[128,2048]{1,0:T(8,128)(2,1)} %subtract_convert_fusion.1) | copy-start | bytes 1572868
  1026.8 637.9 %all-reduce.3.cloned.1.call-start = ((), (), s32[]{:S(2)}) async-start(), calls=%async_computation.18 | async-start | bytes 33554432 | tf_op jit(solution)/shard_map/psum | solution.py:218
  1027.1 9.6 copy-start.22
  1027.1 9.6 copy-start.25
  1036.7 6.2 copy-start.27
  1680.2 6.8 copy-start.13
  1687.0 4.4 copy-start.12
  (10 other events, 13.7 us)
Sparse Core Ops, SparseCore 0:
  9.6 84.7 all-gather.14
  96.0 80.5 all-gather.10
  178.1 80.5 all-gather.8
  261.0 33.6 all-gather.16
  296.9 35.1 all-gather.12
  333.6 82.0 all-gather.18
  422.6 45.3 all-gather.20
  490.3 88.3 reduce-scatter.5
  584.1 45.3 all-gather.22
  656.4 88.3 reduce-scatter.7
  882.6 51.0 reduce-scatter.9
  937.1 52.5 reduce-scatter.11
  1027.0 325.4 reduce-scatter.13
  1357.5 307.2 all-reduce.2
where the time goes:
time: 1720 us; the launch traced here: 1700 us
  waiting for transfers between devices  1230 us (72%)
  matrix products  292 us (17%)
  other arithmetic  69.6 us (4%)
  blocking collectives  54 us (3%)
  local copies, waits for them, and re-layouts  41.3 us (2%)
    reduce_scatter x1, waiting for transfers between devices, shards(): lax.psum_scatter(jnp.concatenate([jnp.dot(tokens_b.T, stacked_in, preferr...  303 us
    psum x1, waiting for transfers between devices, shards(): lax.psum(attn_stack, 'ctx').astype(jnp.float32)  250 us
    reduce_scatter x1, waiting for transfers between devices, shards(): lax.psum_scatter(partial_out, 'fsdp', scatter_dimension=0, tiled=True)  88.4 us
    reduce_scatter x1, waiting for transfers between devices, shards(): lax.psum_scatter(back_part, 'fsdp', scatter_dimension=0, tiled=True)  88.3 us
    all_gather x1, waiting for transfers between devices, shards(): lax.all_gather(w_key, 'fsdp', axis=0, tiled=True)  76.6 us
    all_gather x1, waiting for transfers between devices, shards(): lax.all_gather(w_query, 'fsdp', axis=0, tiled=True)  74.4 us
    all_gather x1, waiting for transfers between devices, shards(): lax.all_gather(w_value, 'fsdp', axis=0, tiled=True)  69 us
    reduce_scatter x1, waiting for transfers between devices, shards(): lax.psum_scatter(grad_value_all, 'ctx', scatter_dimension=0, tiled=True)  52.9 us
  transfers between devices with their start and end apart: 14, of which 14 were waited for; matrix products, arithmetic and copies ran while one was open for 8% of the time, Pallas kernels for 0%

commit v1 on v0

--- a/solution.py
+++ b/solution.py
@@ -209,7 +209,8 @@
         tiled=True,
     )
     gain_stack = jnp.stack([gain_query, gain_key, gain_attn, gain_ff], axis=0)
-    gain_total = lax.psum(gain_stack, ("ctx", "fsdp"))
+    parts = lax.all_gather(gain_stack, ("ctx", "fsdp"), axis=0, tiled=False)
+    gain_total = parts.sum(axis=0)
     gain_width = gain_total.shape[1] // lax.axis_size("fsdp")
     gain_own = lax.dynamic_slice_in_dim(
         gain_total, lax.axis_index("fsdp") * gain_width, gain_width, 1

time: 1720 us -> 1770 us (1.029)
  waiting for transfers between devices: 1230 us -> 1320 us
  blocking collectives: 54 us -> 14.6 us
    psum x1, waiting for transfers between devices: 250 us -> 309 us  [shards(): lax.psum(attn_stack, 'ctx').astype(jnp.float32)]
    psum x1 -> x0, blocking collectives: 39.4 us -> none  [shards(): gain_total = lax.psum(gain_stack, ('ctx', 'fsdp'))]
    all_gather x0 -> x1, waiting for transfers between devices: none -> 34.7 us  [shards(): parts = lax.all_gather(gain_stack, ('ctx', 'fsdp'), axis=0, tiled=False)]
  transfers between devices with their start and end apart: 14 -> 15, of which waited for: 14 -> 15; matrix products, arithmetic and copies ran while one was open for 8% -> 8% of each run, Pallas kernels for 0% -> 0%
where the time goes in v1:
time: 1770 us; the launch traced here: 1760 us
  waiting for transfers between devices  1320 us (75%)
  matrix products  290 us (16%)
  other arithmetic  71.6 us (4%)
  local copies, waits for them, and re-layouts  41.6 us (2%)
    psum x1, waiting for transfers between devices, shards(): lax.psum(attn_stack, 'ctx').astype(jnp.float32)  309 us
    reduce_scatter x1, waiting for transfers between devices, shards(): lax.psum_scatter(jnp.concatenate([jnp.dot(tokens_b.T, stacked_in, preferr...  303 us
    reduce_scatter x1, waiting for transfers between devices, shards(): lax.psum_scatter(partial_out, 'fsdp', scatter_dimension=0, tiled=True)  88.4 us
    reduce_scatter x1, waiting for transfers between devices, shards(): lax.psum_scatter(back_part, 'fsdp', scatter_dimension=0, tiled=True)  88.2 us
    all_gather x1, waiting for transfers between devices, shards(): lax.all_gather(w_key, 'fsdp', axis=0, tiled=True)  76.6 us
    all_gather x1, waiting for transfers between devices, shards(): lax.all_gather(w_query, 'fsdp', axis=0, tiled=True)  74.4 us
    all_gather x1, waiting for transfers between devices, shards(): lax.all_gather(w_value, 'fsdp', axis=0, tiled=True)  69 us
    reduce_scatter x1, waiting for transfers between devices, shards(): lax.psum_scatter(grad_value_all, 'ctx', scatter_dimension=0, tiled=True)  52.9 us
  transfers between devices with their start and end apart: 15, of which 15 were waited for; matrix products, arithmetic and copies ran while one was open for 8% of the time, Pallas kernels for 0%

profile of v1, /device:TPU:0, one launch (start us, length us, event | category | flops | bytes accessed | tf_op | source)
XLA Modules:
  0.0 1757.8 jit_solution(15447227320387927742)
XLA Ops:
  10.3 14.6 all_gather.34
  25.4 69.0 %all-gather.18.cloned.1.call-done = bf16[2048,2048]{1,0:T(8,128)(2,1)} async-done(((bf16[256,2048]{1,0:T(8,128)(2,1)}), bf16[2048,2048]{1,0:T(8,128)(2,1)}) %all-gather.18.cloned.1.call-update) | async-done | bytes 8388624 | tf_op jit(solution)/shard_map/all_gather | solution.py:73
  99.9 76.6 %all-gather.14.cloned.1.call-done = bf16[2048,2048]{1,0:T(8,128)(2,1)} async-done(((bf16[256,2048]{1,0:T(8,128)(2,1)}), bf16[2048,2048]{1,0:T(8,128)(2,1)}) %all-gather.14.cloned.1.call-update) | async-done | bytes 8388624 | tf_op jit(solution)/shard_map/all_gather | solution.py:72
  184.2 74.4 %all-gather.12.cloned.1.call-done = bf16[2048,2048]{1,0:T(8,128)(2,1)} async-done(((bf16[256,2048]{1,0:T(8,128)(2,1)}), bf16[2048,2048]{1,0:T(8,128)(2,1)}) %all-gather.12.cloned.1.call-update) | async-done | bytes 8388624 | tf_op jit(solution)/shard_map/all_gather | solution.py:71
  269.3 25.3 %all-gather.20.cloned.1.call-done = bf16[512,2048]{1,0:T(8,128)(2,1)} async-done(((bf16[128,2048]{1,0:T(8,128)(2,1)}), bf16[512,2048]{1,0:T(8,128)(2,1)}) %all-gather.20.cloned.1.call-update) | async-done | bytes 2097168 | tf_op jit(solution)/shard_map/all_gather | solution.py:95
  298.1 34.0 %all-gather.16.cloned.1.call-done = bf16[512,2048]{1,0:T(8,128)(2,1)} async-done(((bf16[128,2048]{1,0:T(8,128)(2,1)}), bf16[512,2048]{1,0:T(8,128)(2,1)}) %all-gather.16.cloned.1.call-update) | async-done | bytes 2097168 | tf_op jit(solution)/shard_map/all_gather | solution.py:94
  335.6 42.3 %while.28 = (s32[]{:T(128)}, bf16[16,128,128]{1,2,0:T(8,128)(2,1)S(1)}, f32[16,128,1]{1,2,0:T(1,128)S(1)}, bf16[16,128,128]{2,1,0:T(8,128)(2,1)}, bf16[16,512,12...) while((s32[]{:T(128)}, ...), condition=%wide.region_5.6_spmd.clone, body=%wide.region_2.5_spmd.clone.sunk | while | flops 34144128 | bytes 1155689 | solution.py:118
  377.9 37.7 %all-gather.22.cloned.1.call-done = bf16[2048,2048]{1,0:T(8,128)(2,1)} async-done(((bf16[256,2048]{1,0:T(8,128)(2,1)}), bf16[2048,2048]{1,0:T(8,128)(2,1)}) %all-gather.22.cloned.1.call-update) | async-done | bytes 8388624 | tf_op jit(solution)/shard_map/all_gather | solution.py:74
  422.7 45.3 %all-gather.24.cloned.1.call-done = bf16[1024,2048]{1,0:T(8,128)(2,1)} async-done(((bf16[128,2048]{1,0:T(8,128)(2,1)}), bf16[1024,2048]{1,0:T(8,128)(2,1)}) %all-gather.24.cloned.1.call-update) | async-done | bytes 4194320 | tf_op jit(solution)/shard_map/all_gather | solution.py:125
  468.0 7.7 fusion.85
  475.7 6.5 multiply_convert_fusion.3
  483.5 6.7 fusion.86
  490.2 88.4 %reduce-scatter.6.cloned.1.call-done = f32[128,2048]{1,0:T(8,128)} async-done(((f32[1024,2048]{1,0:T(8,128)}), f32[128,2048]{1,0:T(8,128)}) %reduce-scatter.6.cloned.1.call-update) | async-done | bytes 1048592 | tf_op jit(solution)/shard_map/reduce_scatter | solution.py:131
  584.4 45.0 %all-gather.26.cloned.1.call-done = bf16[1024,2048]{1,0:T(8,128)(2,1)} async-done(((bf16[128,2048]{1,0:T(8,128)(2,1)}), bf16[1024,2048]{1,0:T(8,128)(2,1)}) %all-gather.26.cloned.1.call-update) | async-done | bytes 4194320 | tf_op jit(solution)/shard_map/all_gather | solution.py:137
  629.5 13.0 multiply_convert_fusion.1
  642.5 7.0 fusion.87
  649.5 6.8 convolution_add_fusion
  656.6 88.2 %reduce-scatter.8.cloned.1.call-done = f32[128,2048]{1,0:T(8,128)} async-done(((f32[1024,2048]{1,0:T(8,128)}), f32[128,2048]{1,0:T(8,128)}) %reduce-scatter.8.cloned.1.call-update) | async-done | bytes 1048592 | tf_op jit(solution)/shard_map/reduce_scatter | solution.py:144
  750.0 6.5 fusion.56
  757.4 120.3 %while.29 = (s32[]{:T(128)}, f32[16,128,128]{2,1,0:T(8,128)}, f32[16,512,128]{2,1,0:T(8,128)}, f32[16,512,128]{2,1,0:T(8,128)}, bf16[16,128,128]{2,1,0:T(8,128)(...) while((s32[]{:T(128)}, f32[16,128,128]{2,1,0:T(8,128)}, ...), condition=%wide.region_14.15_spmd.clone, body=%wide.region_12.14_spmd.clone.sunk | while | flops 84623232 | bytes 3090561 | solution.py:174
  897.4 36.3 %reduce-scatter.10.cloned.1.call-done = f32[128,2048]{1,0:T(8,128)} async-done(((f32[512,2048]{1,0:T(8,128)}), f32[128,2048]{1,0:T(8,128)}) %reduce-scatter.10.cloned.1.call-update) | async-done | bytes 1048592 | tf_op jit(solution)/shard_map/reduce_scatter | solution.py:181
  936.8 52.9 %reduce-scatter.12.cloned.1.call-done = f32[128,2048]{1,0:T(8,128)} async-done(((f32[512,2048]{1,0:T(8,128)}), f32[128,2048]{1,0:T(8,128)}) %reduce-scatter.12.cloned.1.call-update) | async-done | bytes 1048592 | tf_op jit(solution)/shard_map/reduce_scatter | solution.py:182
  991.0 11.8 convert_bitcast_fusion
  1002.8 23.9 %pad_maximum_fusion = bf16[2048,8192]{0,1:T(8,128)(2,1)} fusion(bf16[2048,2048]{0,1:T(8,128)(2,1)} %convolution_convert_fusion, bf16[2048,6144]{0,1:T(8,128)(2,1)} %convert_bitcast_fusion), kind=kLoop, calls=%fused_computation.57 | loop fusion | flops 67108864 | bytes 67108864 | tf_op jit(solution)/shard_map/concatenate | solution.py:200
  1027.7 9.6 convolution_convert_fusion.1
  1049.8 302.6 %reduce-scatter.14.cloned.1.call-done = bf16[256,8192]{0,1:T(8,128)(2,1)} async-done(((bf16[2048,8192]{0,1:T(8,128)(2,1)}), bf16[256,8192]{0,1:T(8,128)(2,1)}) %reduce-scatter.14.cloned.1.call-update) | async-done | bytes 4194320 | tf_op jit(solution)/shard_map/reduce_scatter | solution.py:199
  1353.6 6.3 convolution_add_fusion.3
  1359.8 6.3 convolution_add_fusion.2
  1366.2 7.3 fusion.48
  1373.4 34.7 %all-gather.28.cloned.1.call-done = f32[32,4,2048]{2,1,0:T(4,128)} async-done(((f32[1,4,2048]{2,1,0:T(4,128)}), f32[32,4,2048]{2,1,0:T(4,128)}) %all-gather.28.cloned.1.call-update) | async-done | bytes 1048592 | tf_op jit(solution)/shard_map/all_gather | solution.py:212
  1410.1 309.4 %all-reduce.3.cloned.1.call-done = (bf16[256,8192]{0,1:T(8,128)(2,1)}, bf16[2048,1024]{1,0:T(8,128)(2,1)}, bf16[2048,1024]{1,0:T(8,128)(2,1)}, bf16[1024,2048]{1,0:T(8,128)(2,1)}) async-done(((bf16[256,8192]{0,1:T(8,128)(2,1)}, bf16[2048,1024]{1,0:T(8,128)(2,1)}, bf16[2048,1024]{1,0:T(8,128)(2,1)}, bf16[1024,2048]{1,0:T(8,128)(2,1)}), (bf16[256,8192]{0,1:T(8,128)(2,1)}, bf16[2048,1024]{1,0:T(8,128)(2,1)}, ...) | async-done | bytes 16777232 | tf_op jit(solution)/shard_map/psum | solution.py:219
  1735.2 6.8 convert_element_type.122
  (329 shorter events, 281.8 us)
Async XLA Ops:
  7.2 87.2 %copy-start = (bf16[1,128,2048]{2,1,0:T(8,128)(2,1)S(1)}, bf16[1,128,2048]{2,1,0:T(8,128)(2,1)}, u32[]{:S(2)}) copy-start(bf16[1,128,2048]{2,1,0:T(8,128)(2,1)} %param.15) | copy-start | bytes 1572868
  7.2 87.2 %all-gather.18.cloned.1.call-start = ((), (), s32[]{:S(2)}) async-start(), calls=%async_computation.8 | async-start | bytes 9437184 | tf_op jit(solution)/shard_map/all_gather | solution.py:73
  7.9 168.6 %all-gather.14.cloned.1.call-start = ((), (), s32[]{:S(2)}) async-start(), calls=%async_computation.6 | async-start | bytes 9437184 | tf_op jit(solution)/shard_map/all_gather | solution.py:72
  8.7 250.0 %all-gather.12.cloned.1.call-start = ((), (), s32[]{:S(2)}) async-start(), calls=%async_computation.5 | async-start | bytes 9437184 | tf_op jit(solution)/shard_map/all_gather | solution.py:71
  9.4 285.3 %all-gather.20.cloned.1.call-start = ((), (), s32[]{:S(2)}) async-start(), calls=%async_computation.9 | async-start | bytes 2621440 | tf_op jit(solution)/shard_map/all_gather | solution.py:95
  99.8 232.3 %all-gather.16.cloned.1.call-start = ((), (), s32[]{:S(2)}) async-start(), calls=%async_computation.7 | async-start | bytes 2621440 | tf_op jit(solution)/shard_map/all_gather | solution.py:94
  258.7 5.0 copy-start.16
  268.7 147.0 %all-gather.22.cloned.1.call-start = ((), (), s32[]{:S(2)}) async-start(), calls=%async_computation.10 | async-start | bytes 9437184 | tf_op jit(solution)/shard_map/all_gather | solution.py:74
  269.3 198.7 %all-gather.24.cloned.1.call-start = ((), (), s32[]{:S(2)}) async-start(), calls=%async_computation.11 | async-start | bytes 4718592 | tf_op jit(solution)/shard_map/all_gather | solution.py:125
  377.9 42.5 %copy-start.10 = (bf16[16,128,128]{1,2,0:T(8,128)(2,1)}, bf16[16,128,128]{1,2,0:T(8,128)(2,1)S(1)}, u32[]{:S(2)}) copy-start(bf16[16,128,128]{1,2,0:T(8,128)(2,1)S(1)} %get-tuple-element.102) | copy-start | bytes 1572868
  422.4 156.2 %reduce-scatter.6.cloned.1.call-start = ((), (), s32[]{:S(2)}) async-start(), calls=%async_computation.12 | async-start | bytes 9437184 | tf_op jit(solution)/shard_map/reduce_scatter | solution.py:131
  468.0 7.7 copy-start.19
  468.0 7.7 copy-start.21
  475.7 6.5 copy-start.26
  475.7 7.8 copy-start.17
  490.2 89.9 %copy-start.2 = (bf16[1,128,2048]{2,1,0:T(8,128)(2,1)S(1)}, bf16[1,128,2048]{2,1,0:T(8,128)(2,1)}, u32[]{:S(2)}) copy-start(bf16[1,128,2048]{2,1,0:T(8,128)(2,1)} %param.25) | copy-start | bytes 1572868
  490.2 139.3 %all-gather.26.cloned.1.call-start = ((), (), s32[]{:S(2)}) async-start(), calls=%async_computation.13 | async-start | bytes 4718592 | tf_op jit(solution)/shard_map/all_gather | solution.py:137
  584.0 160.8 %reduce-scatter.8.cloned.1.call-start = ((), (), s32[]{:S(2)}) async-start(), calls=%async_computation.14 | async-start | bytes 9437184 | tf_op jit(solution)/shard_map/reduce_scatter | solution.py:144
  629.5 13.0 copy-start.18
  642.5 7.0 copy-start.24
  642.5 7.0 copy-start.20
  656.3 277.3 %reduce-scatter.10.cloned.1.call-start = ((), (), s32[]{:S(2)}) async-start(), calls=%async_computation.15 | async-start | bytes 5242880 | tf_op jit(solution)/shard_map/reduce_scatter | solution.py:181
  750.0 6.5 copy-start.8
  882.4 107.2 %reduce-scatter.12.cloned.1.call-start = ((), (), s32[]{:S(2)}) async-start(), calls=%async_computation.16 | async-start | bytes 5242880 | tf_op jit(solution)/shard_map/reduce_scatter | solution.py:182
  887.3 465.0 %reduce-scatter.14.cloned.1.call-start = ((), (), s32[]{:S(2)}) async-start(), calls=%async_computation.17 | async-start | bytes 37748736 | tf_op jit(solution)/shard_map/reduce_scatter | solution.py:199
  935.5 55.4 %copy-start.7 = (bf16[128,2048]{1,0:T(8,128)(2,1)S(1)}, bf16[128,2048]{1,0:T(8,128)(2,1)}, u32[]{:S(2)}) copy-start(bf16[128,2048]{1,0:T(8,128)(2,1)} %subtract_convert_fusion.1) | copy-start | bytes 1572868
  1026.7 381.4 %all-gather.28.cloned.1.call-start = ((), (), s32[]{:S(2)}) async-start(), calls=%async_computation.18 | async-start | bytes 1081344 | tf_op jit(solution)/shard_map/all_gather | solution.py:212
  1027.5 692.0 %all-reduce.3.cloned.1.call-start = ((), (), s32[]{:S(2)}) async-start(), calls=%async_computation.19 | async-start | bytes 33554432 | tf_op jit(solution)/shard_map/psum | solution.py:219
  1027.7 9.6 copy-start.22
  1027.7 9.6 copy-start.25
  1037.3 6.2 copy-start.27
  1735.2 6.8 copy-start.13
  (11 other events, 18.2 us)
Sparse Core Ops, SparseCore 0:
  9.6 84.7 all-gather.17
  96.0 80.5 all-gather.13
  178.1 80.5 all-gather.11
  261.0 33.6 all-gather.19
  296.9 35.1 all-gather.15
  333.6 82.0 all-gather.21
  422.6 45.3 all-gather.23
  490.3 88.3 reduce-scatter.5
  584.1 45.3 all-gather.25
  656.4 88.3 reduce-scatter.7
  882.6 51.0 reduce-scatter.9
  937.0 52.5 reduce-scatter.11
  1026.8 325.4 reduce-scatter.13
  1355.8 52.2 all-gather.27
  1413.1 306.3 all-reduce.2
